TPU v7x, 256 devices: a whole 4x4x8 slice. The times are simulated.
256 devices in a mesh: row: 32 (over y, z), col: 8 (over x, core).
Axes of the slice: x: 4, y: 4, z: 8, core: 2. Of those that a mesh axis runs over, the one named last changes fastest.
Arguments:
- grams: bfloat16 [4, 3584, 3584], P(None, 'row', 'col'), as said below
- weights: bfloat16 [4, 3584, 7168], P(None, 'row', 'col'), may hold values from -6 to 6
Outputs:
- merged: float32 [3584, 7168], P('row', 'col')
- residual: float32 [3584, 7168], P('row', 'col')
Inputs may be any that keep to these rules, and one draw needn't show every extreme that they name: `grams`: each of the 4 matrices is symmetric and positive definite.
All inputs are finite; a program needn't handle non-finite values.
Results may differ from a plain program's by a relative error of at most 0.012.
The roundings to bfloat16 on the way count: a program that leaves them out, or rounds other values in their place, can miss the bound.
Values may be sent and summed in bfloat16 or wider, within the bound.
A program may use at most 256 MiB of HBM per device.

v0:
```python
import jax
import jax.numpy as jnp
from jax import lax
from jax.sharding import Mesh
from jax.sharding import PartitionSpec as P

ITERS = 2
ROW = ("row_0", "row_1")


def sum_by_axis(so_far, axes):
    for axis in axes:
        so_far = lax.psum_scatter(so_far, axis, scatter_dimension=0, tiled=True)
    return so_far


def sent_to_all(x, axis):
    copies = jnp.broadcast_to(x, (lax.axis_size(axis), *x.shape))
    return lax.all_to_all(copies, axis, split_axis=0, concat_axis=0, tiled=True)


def of_everyone(x, axis):
    return sent_to_all(x, axis).sum(axis=0)


def together(arrays, axis):
    ravelled, at, done = (jnp.concatenate([a.reshape(-1) for a in arrays]), 0, [])
    so_far = of_everyone(ravelled, axis)
    for a in arrays:
        done.append(so_far[at : at + a.size].reshape(a.shape))
        at += a.size
    return tuple(done)


def shards(grams, weights):
    slab_rows = grams.shape[1]
    col_count = weights.shape[2]
    first_row = lax.axis_index(ROW) * slab_rows
    high = lax.Precision.HIGHEST
    gram_slabs = lax.all_gather(grams, "col", axis=2, tiled=True)
    gram_total = jnp.sum(gram_slabs, axis=0, dtype=jnp.float32)
    square_block = lax.dynamic_slice_in_dim(gram_slabs, first_row, slab_rows, gram_slabs.ndim - 1)
    diag_total = jnp.einsum(
        "mr,mrc->rc",
        jnp.diagonal(square_block, axis1=-2, axis2=-1).astype(jnp.float32),
        weights.astype(jnp.float32),
    )
    product = sum_by_axis(
        jnp.einsum("mrk,mrc->kc", gram_slabs, weights, preferred_element_type=jnp.float32), ROW
    )
    right_side = 0.9 * product + 0.1 * diag_total
    total_diag = jnp.diagonal(lax.dynamic_slice_in_dim(gram_total, first_row, slab_rows, 1))
    merged = jnp.zeros((slab_rows, col_count), jnp.float32)
    residual = right_side
    direction = right_side
    for iteration in range(ITERS):
        rounded = direction.astype(jnp.bfloat16)
        shard_piece = lax.all_gather(rounded, ROW, axis=0, tiled=True)
        add_columns = lax.slice_in_dim(gram_total, 0, shard_piece.shape[0], axis=1)
        mapped = jnp.zeros((slab_rows, col_count), jnp.float32) + jnp.dot(
            add_columns, shard_piece.astype(jnp.float32), precision=high
        )
        mapped = 0.9 * mapped + 0.1 * total_diag[:, None] * rounded.astype(jnp.float32)
        curvature, cross_term, square, norm_now = together(
            (
                jnp.sum(direction * mapped, axis=0),
                jnp.sum(residual * mapped, axis=0),
                jnp.sum(mapped * mapped, axis=0),
                jnp.sum(residual * residual, axis=0),
            ),
            ROW,
        )
        step_length = norm_now / curvature
        merged = merged + step_length * direction
        residual = residual - step_length * mapped
        if iteration + 1 < ITERS:
            norm_next = (
                norm_now - 2.0 * step_length * cross_term + step_length * step_length * square
            )
            direction = residual + norm_next / norm_now * direction
    return (merged, residual)


def solution(mesh):
    torus = Mesh(mesh.devices.reshape(4, 8, mesh.shape["col"]), ("row_0", "row_1", "col"))
    in_specs = (P(None, ROW, "col"), P(None, ROW, "col"))
    out_specs = (P(ROW, "col"), P(ROW, "col"))
    return jax.shard_map(
        shards, mesh=torus, in_specs=in_specs, out_specs=out_specs, check_vma=False
    )
```

profile of v0, /device:TPU:32, one launch (start us, length us, event | category | flops | bytes accessed | tf_op | source)
XLA Modules:
  0.0 467.3 jit_solution(11836406161750740182)
XLA Ops:
  7.2 0.0 all-gather.4.cloned.1.call-start
  7.2 2.1 copy.14
  9.3 0.0 all-gather.4.cloned.1.call-update
  9.3 0.0 reduce-scatter.3.cloned.1.call-start
  9.4 35.5 %all-gather.4.cloned.1.call-done = bf16[4,112,3584]{1,2,0:T(8,128)(2,1)} async-done(((bf16[4,112,448]{1,2,0:T(8,128)(2,1)}), bf16[4,112,3584]{1,2,0:T(8,128)(2,1)}) %all-gather.4.cloned.1.call-update) | async-done | bytes 3211280 | tf_op jit(solution)/shard_map/all_gather | solution.py:40
  44.9 8.9 %convolution_bitcast_fusion = f32[3584,896]{1,0:T(8,128)} fusion(bf16[4,112,3584]{1,2,0:T(8,128)(2,1)} %all-gather.4.cloned.1.call-done, bf16[4,112,896]{2,1,0:T(8,128)(2,1)S(1)} %copy-done), kind=kOutput, calls=%fused_computation.2 | convolution fusion | flops 2877292544 | bytes 16859136 | tf_op jit(solution)/shard_map/mrk,mrc->kc/dot_general | solution.py:49
  53.7 0.0 reduce-scatter.3.cloned.1.call-update
  53.8 0.0 reduce-scatter.5.cloned.1.call-start
  53.8 119.3 %reduce-scatter.3.cloned.1.call-done = f32[896,896]{1,0:T(8,128)} async-done(((f32[3584,896]{1,0:T(8,128)}), f32[896,896]{1,0:T(8,128)}) %reduce-scatter.3.cloned.1.call-update) | async-done | bytes 3211280 | tf_op jit(solution)/shard_map/reduce_scatter | solution.py:13
  173.1 0.0 all-gather.6.cloned.1.call-start
  173.2 0.9 constant_dynamic-slice_fusion.1
  174.1 3.2 copy.15
  177.3 2.9 gather_fusion
  180.2 0.6 fusion.2
  180.8 41.3 %reduce-scatter.5.cloned.1.call-done = f32[112,896]{1,0:T(8,128)} async-done(((f32[896,896]{1,0:T(8,128)}), f32[112,896]{1,0:T(8,128)}) %reduce-scatter.5.cloned.1.call-update) | async-done | bytes 401424 | tf_op jit(solution)/shard_map/reduce_scatter | solution.py:13
  222.1 1.8 fusion.10
  223.9 0.0 all-gather.8.cloned.1.call-start
  223.9 3.0 convert_reduce_fusion
  227.0 0.1 copy.24
  227.1 1.7 gather_fusion.1
  228.8 85.2 %all-gather.6.cloned.1.call-done = bf16[3584,896]{1,0:T(8,128)(2,1)} async-done(((bf16[112,896]{1,0:T(8,128)(2,1)}), bf16[3584,896]{1,0:T(8,128)(2,1)}) %all-gather.6.cloned.1.call-update) | async-done | bytes 6422544 | tf_op jit(solution)/shard_map/all_gather | solution.py:58
  314.0 7.0 %multiply_reduce_fusion.6 = (f32[896]{0:T(1024)S(1)}, f32[896]{0:T(1024)S(1)}, f32[896]{0:T(1024)S(1)}, f32[112,896]{1,0:T(8,128)}) fusion(f32[112,896]{1,0:T(8,128)S(1)} %get-tuple-element.14, bf16[112,896]{1,0:T(8,128)(2,1)S(1)} %copy-done.1, f32[112]{0:T(128)S(1)} %broadcast_multiply_fusion, f32[112,3584]{0,1:T(8,128)S(1)} %convert_reduce_fusion, ...), kind=kOutput, calls=%fused_computation.22 | convolution fusion | flops 4316939776 | bytes 9042880 | tf_op jit(solution)/shard_map/dot_general | solution.py:60
  320.9 0.2 broadcast_in_dim.12
  321.2 21.5 %all_to_all.12 = f32[32,1,3584]{2,1,0:T(1,128)S(1)} all-to-all(f32[32,1,3584]{2,1,0:T(1,128)S(1)} %broadcast_in_dim.12), channel_id=1, replica_groups=mesh['row_0'=4,'row_1'=8,'col'=8] {'row_0','row_1'}, dimensions={0} | all-to-all | bytes 917504 | tf_op jit(solution)/shard_map/all_to_all | solution.py:19
  342.7 0.3 reduce_sum.98
  343.0 1.7 fusion.5
  344.8 84.9 %all-gather.8.cloned.1.call-done = bf16[3584,896]{1,0:T(8,128)(2,1)} async-done(((bf16[112,896]{1,0:T(8,128)(2,1)}), bf16[3584,896]{1,0:T(8,128)(2,1)}) %all-gather.8.cloned.1.call-update) | async-done | bytes 6422544 | tf_op jit(solution)/shard_map/all_gather | solution.py:58
  429.7 7.0 %multiply_reduce_fusion.3 = (f32[896]{0:T(1024)S(1)}, f32[896]{0:T(1024)S(1)}, f32[896]{0:T(1024)S(1)}, f32[896]{0:T(1024)S(1)}, f32[112,896]{1,0:T(8,128)}) fusion(f32[112,896]{1,0:T(8,128)S(1)} %get-tuple-element.10, f32[112,896]{1,0:T(8,128)S(1)} %get-tuple-element.14, f32[896]{0:T(1024)S(1)} %get-tuple-element.11, ...), kind=kOutput, calls=%fused_computation.17 | convolution fusion | flops 4317340160 | bytes 9451456 | tf_op jit(solution)/shard_map/dot_general | solution.py:60
  436.7 0.2 broadcast_in_dim.13
  437.0 21.5 %all_to_all.13 = f32[32,1,3584]{2,1,0:T(1,128)S(1)} all-to-all(f32[32,1,3584]{2,1,0:T(1,128)S(1)} %broadcast_in_dim.13), channel_id=1, replica_groups=mesh['row_0'=4,'row_1'=8,'col'=8] {'row_0','row_1'}, dimensions={0} | all-to-all | bytes 917504 | tf_op jit(solution)/shard_map/all_to_all | solution.py:19
  458.5 0.3 reduce_sum.103
  458.8 2.0 multiply_subtract_fusion
  (14 shorter events, 0.1 us)
Async XLA Ops:
  7.2 37.7 %copy-start = (bf16[4,112,896]{2,1,0:T(8,128)(2,1)S(1)}, bf16[4,112,896]{2,1,0:T(8,128)(2,1)}, u32[]{:S(2)}) copy-start(bf16[4,112,896]{2,1,0:T(8,128)(2,1)} %param.3) | copy-start | bytes 2408452
  7.2 37.7 %all-gather.4.cloned.1.call-start = ((), (), s32[]{:S(2)}) async-start(), calls=%async_computation.4 | async-start | bytes 4128768 | tf_op jit(solution)/shard_map/all_gather | solution.py:40
  9.3 163.8 %reduce-scatter.3.cloned.1.call-start = ((), (), s32[]{:S(2)}) async-start(), calls=%async_computation.5 | async-start | bytes 16056320 | tf_op jit(solution)/shard_map/reduce_scatter | solution.py:13
  53.8 168.3 %reduce-scatter.5.cloned.1.call-start = ((), (), s32[]{:S(2)}) async-start(), calls=%async_computation.6 | async-start | bytes 3612672 | tf_op jit(solution)/shard_map/reduce_scatter | solution.py:13
  173.1 140.9 %all-gather.6.cloned.1.call-start = ((), (), s32[]{:S(2)}) async-start(), calls=%async_computation.7 | async-start | bytes 6623232 | tf_op jit(solution)/shard_map/all_gather | solution.py:58
  223.9 90.1 %copy-start.1 = (bf16[112,896]{1,0:T(8,128)(2,1)S(1)}, bf16[112,896]{1,0:T(8,128)(2,1)}, u32[]{:S(2)}) copy-start(bf16[112,896]{1,0:T(8,128)(2,1)} %get-tuple-element.13) | copy-start | bytes 602116
  223.9 205.8 %all-gather.8.cloned.1.call-start = ((), (), s32[]{:S(2)}) async-start(), calls=%async_computation.8 | async-start | bytes 6623232 | tf_op jit(solution)/shard_map/all_gather | solution.py:58
Sparse Core Ops, SparseCore 0:
  9.8 34.9 all-gather.3
  53.9 119.1 reduce-scatter.2
  175.6 46.4 reduce-scatter.4
  225.1 88.8 all-gather.5
  344.9 84.7 all-gather.7
where the time goes:
time: 468 us; the launch traced here: 467 us
  waiting for transfers between devices  366 us (78%)
  blocking collectives  43.1 us (9%)
  matrix products  23.4 us (5%)
  between operations  13.9 us (3%)
  local copies, waits for them, and re-layouts  11.4 us (2%)
  other arithmetic  9.11 us (2%)
    all_gather x2, waiting for transfers between devices, shards(): shard_piece = lax.all_gather(rounded, ROW, axis=0, tiled=True)  170 us
    reduce_scatter x2, waiting for transfers between devices, sum_by_axis(): so_far = lax.psum_scatter(so_far, axis, scatter_dimension=0, tiled=True)  161 us
    all_to_all x2, blocking collectives, sent_to_all(): return lax.all_to_all(copies, axis, split_axis=0, concat_axis=0, tiled=True)  43.1 us
    all_gather x1, waiting for transfers between devices, shards(): gram_slabs = lax.all_gather(grams, 'col', axis=2, tiled=True)  35.5 us
    dot_general x2, matrix products, shards(): jnp.dot(add_columns, shard_piece.astype(jnp.float32), precision=high)  14 us
  transfers between devices with their start and end apart: 5, of which 5 were waited for; matrix products, arithmetic and copies ran while one was open for 3% of the time, Pallas kernels for 0%

commit v1 on v0

--- a/solution.py
+++ b/solution.py
@@ -3,6 +3,7 @@
 from jax import lax
 from jax.sharding import Mesh
 from jax.sharding import PartitionSpec as P
+from jax.lax import axis_index, axis_size, ppermute
 
 ITERS = 2
 ROW = ("row_0", "row_1")
@@ -33,11 +34,43 @@
 
 
 def shards(grams, weights):
+
+    def mix_the_knots(state, net_axis="col"):
+        lower, mid_arr, oldest = (axis_size(net_axis), axis_index(net_axis), state.shape[2])
+        gallery = []
+        for nth, dev in enumerate(state.shape):
+            gallery.append(dev * lower if nth == 2 else dev)
+        aux = lax.dynamic_update_slice_in_dim(
+            jnp.zeros(gallery, state.dtype), state, mid_arr * oldest, axis=2
+        )
+        val = f_now = state
+        pp = 1
+        while pp < lower // 2 + 1:
+            crops = []
+            nth = 0
+            while nth < lower:
+                crops.append((nth, (nth + 1) % lower))
+                nth += 1
+            val = ppermute(val, axis_name=net_axis, perm=crops)
+            aux = lax.dynamic_update_slice_in_dim(aux, val, (mid_arr - pp) % lower * oldest, axis=2)
+            if 2 * pp < lower:
+                tray = []
+                nth = 0
+                while nth < lower:
+                    tray.append((nth, (nth - 1) % lower))
+                    nth += 1
+                f_now = ppermute(f_now, axis_name=net_axis, perm=tray)
+                aux = lax.dynamic_update_slice_in_dim(
+                    aux, f_now, (mid_arr + pp) % lower * oldest, axis=2
+                )
+            pp += 1
+        return aux
+
     slab_rows = grams.shape[1]
     col_count = weights.shape[2]
     first_row = lax.axis_index(ROW) * slab_rows
     high = lax.Precision.HIGHEST
-    gram_slabs = lax.all_gather(grams, "col", axis=2, tiled=True)
+    gram_slabs = mix_the_knots(grams)
     gram_total = jnp.sum(gram_slabs, axis=0, dtype=jnp.float32)
     square_block = lax.dynamic_slice_in_dim(gram_slabs, first_row, slab_rows, gram_slabs.ndim - 1)
     diag_total = jnp.einsum(

time: 468 us -> 718 us (1.53)
  local copies, waits for them, and re-layouts: 11.4 us -> 283 us
  waiting for transfers between devices: 366 us -> 303 us
  other arithmetic: 9.11 us -> 39.7 us
  starting transfers between devices: 0.2 us -> 9.1 us
    dynamic_update_slice x0 -> x9, local copies, waits for them, and re-layouts: none -> 159 us  [the longest x5 121 us: mix_the_knots(): lax.dynamic_update_slice_in_dim(aux, val, (mid_arr - pp) % lower * oldest...]
    ppermute x0 -> x7, local copies, waits for them, and re-layouts: none -> 69.3 us  [the longest x4 39.6 us: mix_the_knots(): val = ppermute(val, axis_name=net_axis, perm=crops)]
    all_gather x1 -> x0, waiting for transfers between devices: 35.5 us -> none  [shards(): gram_slabs = lax.all_gather(grams, 'col', axis=2, tiled=True)]
    broadcast_in_dim x0 -> x1, local copies, waits for them, and re-layouts: none -> 35.4 us  [mix_the_knots(): jnp.zeros(gallery, state.dtype)]
    all_gather x2, waiting for transfers between devices: 170 us -> 139 us  [shards(): shard_piece = lax.all_gather(rounded, ROW, axis=0, tiled=True)]
    reduce_sum x1, other arithmetic: 3.03 us -> 33.7 us  [shards(): gram_total = jnp.sum(gram_slabs, axis=0, dtype=jnp.float32)]
    ppermute x0 -> x7, starting transfers between devices: none -> 8.76 us  [the longest x3 8.74 us: mix_the_knots(): f_now = ppermute(f_now, axis_name=net_axis, perm=tray)]
    unnamed x6 -> x7, local copies, waits for them, and re-layouts: 2.16 us -> 10.9 us
  transfers between devices with their start and end apart: 5 -> 11, of which waited for: 5 -> 4; matrix products, arithmetic and copies ran while one was open for 3% -> 31% of each run, Pallas kernels for 0% -> 0%
where the time goes in v1:
time: 718 us; the launch traced here: 715 us
  waiting for transfers between devices  303 us (42%)
  local copies, waits for them, and re-layouts  283 us (39%)
  blocking collectives  43.1 us (6%)
  other arithmetic  39.7 us (6%)
  matrix products  22.7 us (3%)
  between operations  13.9 us (2%)
  starting transfers between devices  9.1 us (1%)
    reduce_scatter x2, waiting for transfers between devices, sum_by_axis(): so_far = lax.psum_scatter(so_far, axis, scatter_dimension=0, tiled=True)  164 us
    all_gather x2, waiting for transfers between devices, shards(): shard_piece = lax.all_gather(rounded, ROW, axis=0, tiled=True)  139 us
    dynamic_update_slice x5, local copies, waits for them, and re-layouts, mix_the_knots(): lax.dynamic_update_slice_in_dim(aux, val, (mid_arr - pp) % lower * oldest...  121 us
    all_to_all x2, blocking collectives, sent_to_all(): return lax.all_to_all(copies, axis, split_axis=0, concat_axis=0, tiled=True)  43.1 us
    ppermute x4, local copies, waits for them, and re-layouts, mix_the_knots(): val = ppermute(val, axis_name=net_axis, perm=crops)  39.6 us
    broadcast_in_dim x1, local copies, waits for them, and re-layouts, mix_the_knots(): jnp.zeros(gallery, state.dtype)  35.4 us
    reduce_sum x1, other arithmetic, shards(): gram_total = jnp.sum(gram_slabs, axis=0, dtype=jnp.float32)  33.7 us
    dynamic_update_slice x3, local copies, waits for them, and re-layouts, mix_the_knots(): lax.dynamic_update_slice_in_dim(aux, f_now, (mid_arr + pp) % lower * olde...  32.2 us
  transfers between devices with their start and end apart: 11, of which 4 were waited for; matrix products, arithmetic and copies ran while one was open for 31% of the time, Pallas kernels for 0%

profile of v1, /device:TPU:32, one launch (start us, length us, event | category | flops | bytes accessed | tf_op | source)
XLA Modules:
  0.0 715.0 jit_solution(9014105755771254379)
XLA Ops:
  7.2 2.9 collective-permute-start.1
  10.2 10.8 %copy.30 = bf16[4,112,448]{0,2,1:T(8,128)(2,1)} copy(bf16[4,112,448]{2,1,0:T(8,128)(2,1)} %param.2) | data formatting | bytes 802816 | tf_op args[0]
  21.0 35.4 %broadcast_in_dim.14 = bf16[4,112,3584]{0,2,1:T(8,128)(2,1)} broadcast(bf16[]{:T(256)} %constant.70.clone.1), dimensions={} | broadcast | bytes 3211266 | tf_op jit(solution)/shard_map/broadcast_in_dim | solution.py:44
  56.4 5.4 constant_dynamic-update-slice_fusion.7
  61.8 9.9 %copy.31 = bf16[4,112,448]{0,2,1:T(8,128)(2,1)} copy(bf16[4,112,448]{2,1,0:T(8,128)(2,1)S(1)} %collective-permute-done) | data formatting | bytes 802816 | tf_op jit(solution)/shard_map/ppermute | solution.py:54
  71.7 10.7 %constant_dynamic-update-slice_fusion.6 = bf16[4,112,3584]{0,2,1:T(8,128)(2,1)} fusion(bf16[4,112,3584]{0,2,1:T(8,128)(2,1)} %constant_dynamic-update-slice_fusion.7, bf16[4,112,448]{0,2,1:T(8,128)(2,1)} %copy.31, s32[]{:T(128)S(6)} %select_n.69), kind=kLoop, calls=%fused_computation.42 | loop fusion | bytes 25690116 | tf_op jit(solution)/shard_map/dynamic_update_slice | solution.py:55
  82.4 9.9 %copy.32 = bf16[4,112,448]{0,2,1:T(8,128)(2,1)} copy(bf16[4,112,448]{2,1,0:T(8,128)(2,1)S(1)} %collective-permute-done.1) | data formatting | bytes 802816 | tf_op jit(solution)/shard_map/ppermute | solution.py:62
  92.3 10.6 %constant_dynamic-update-slice_fusion.5 = bf16[4,112,3584]{0,2,1:T(8,128)(2,1)} fusion(bf16[4,112,3584]{0,2,1:T(8,128)(2,1)} %constant_dynamic-update-slice_fusion.6, bf16[4,112,448]{0,2,1:T(8,128)(2,1)} %copy.32, s32[]{:T(128)S(6)} %select_n.71), kind=kLoop, calls=%fused_computation.41 | loop fusion | bytes 25690116 | tf_op jit(solution)/shard_map/dynamic_update_slice | solution.py:63
  103.0 3.0 collective-permute-start.3
  106.0 9.9 %copy.33 = bf16[4,112,448]{0,2,1:T(8,128)(2,1)} copy(bf16[4,112,448]{2,1,0:T(8,128)(2,1)S(1)} %collective-permute-done.2) | data formatting | bytes 802816 | tf_op jit(solution)/shard_map/ppermute | solution.py:54
  115.9 10.7 %constant_dynamic-update-slice_fusion.4 = bf16[4,112,3584]{0,2,1:T(8,128)(2,1)} fusion(bf16[4,112,3584]{0,2,1:T(8,128)(2,1)} %constant_dynamic-update-slice_fusion.5, bf16[4,112,448]{0,2,1:T(8,128)(2,1)} %copy.33, s32[]{:T(128)S(6)} %select_n.73), kind=kLoop, calls=%fused_computation.40 | loop fusion | bytes 25690116 | tf_op jit(solution)/shard_map/dynamic_update_slice | solution.py:55
  126.6 9.9 %copy.34 = bf16[4,112,448]{0,2,1:T(8,128)(2,1)} copy(bf16[4,112,448]{2,1,0:T(8,128)(2,1)S(1)} %collective-permute-done.3) | data formatting | bytes 802816 | tf_op jit(solution)/shard_map/ppermute | solution.py:62
  136.6 10.8 %constant_dynamic-update-slice_fusion.3 = bf16[4,112,3584]{0,2,1:T(8,128)(2,1)} fusion(bf16[4,112,3584]{0,2,1:T(8,128)(2,1)} %constant_dynamic-update-slice_fusion.4, bf16[4,112,448]{0,2,1:T(8,128)(2,1)} %copy.34, s32[]{:T(128)S(6)} %select_n.75), kind=kLoop, calls=%fused_computation.39 | loop fusion | bytes 25690116 | tf_op jit(solution)/shard_map/dynamic_update_slice | solution.py:63
  150.1 9.9 %copy.35 = bf16[4,112,448]{0,2,1:T(8,128)(2,1)} copy(bf16[4,112,448]{2,1,0:T(8,128)(2,1)S(1)} %collective-permute-done.4) | data formatting | bytes 802816 | tf_op jit(solution)/shard_map/ppermute | solution.py:54
  160.0 10.7 %constant_dynamic-update-slice_fusion.2 = bf16[4,112,3584]{0,2,1:T(8,128)(2,1)} fusion(bf16[4,112,3584]{0,2,1:T(8,128)(2,1)} %constant_dynamic-update-slice_fusion.3, bf16[4,112,448]{0,2,1:T(8,128)(2,1)} %copy.35, s32[]{:T(128)S(6)} %select_n.77), kind=kLoop, calls=%fused_computation.38 | loop fusion | bytes 25690116 | tf_op jit(solution)/shard_map/dynamic_update_slice | solution.py:55
  170.8 9.9 %copy.36 = bf16[4,112,448]{0,2,1:T(8,128)(2,1)} copy(bf16[4,112,448]{2,1,0:T(8,128)(2,1)S(1)} %collective-permute-done.5) | data formatting | bytes 802816 | tf_op jit(solution)/shard_map/ppermute | solution.py:62
  180.7 10.8 %constant_dynamic-update-slice_fusion.1 = bf16[4,112,3584]{0,2,1:T(8,128)(2,1)} fusion(bf16[4,112,3584]{0,2,1:T(8,128)(2,1)} %constant_dynamic-update-slice_fusion.2, bf16[4,112,448]{0,2,1:T(8,128)(2,1)} %copy.36, s32[]{:T(128)S(6)} %select_n.79), kind=kLoop, calls=%fused_computation.37 | loop fusion | bytes 25690116 | tf_op jit(solution)/shard_map/dynamic_update_slice | solution.py:63
  191.5 9.9 %copy.37 = bf16[4,112,448]{0,2,1:T(8,128)(2,1)} copy(bf16[4,112,448]{2,1,0:T(8,128)(2,1)S(1)} %collective-permute-done.6) | data formatting | bytes 802816 | tf_op jit(solution)/shard_map/ppermute | solution.py:54
  201.4 10.7 %constant_dynamic-update-slice_fusion = bf16[4,112,3584]{0,2,1:T(8,128)(2,1)} fusion(bf16[4,112,3584]{0,2,1:T(8,128)(2,1)} %constant_dynamic-update-slice_fusion.1, bf16[4,112,448]{0,2,1:T(8,128)(2,1)} %copy.37, s32[]{:T(128)S(6)} %select_n.81), kind=kLoop, calls=%fused_computation.36 | loop fusion | bytes 25690116 | tf_op jit(solution)/shard_map/dynamic_update_slice | solution.py:55
  212.1 78.5 %copy.38 = bf16[4,112,3584]{2,1,0:T(8,128)(2,1)} copy(bf16[4,112,3584]{0,2,1:T(8,128)(2,1)} %constant_dynamic-update-slice_fusion) | data formatting | bytes 6422528 | tf_op jit(solution)/shard_map/dynamic_update_slice | solution.py:55
  290.6 8.8 %convolution_bitcast_fusion = f32[3584,896]{1,0:T(8,128)} fusion(bf16[4,112,3584]{2,1,0:T(8,128)(2,1)} %copy.38, bf16[4,112,896]{2,1,0:T(8,128)(2,1)S(1)} %copy-done), kind=kOutput, calls=%fused_computation.3 | convolution fusion | flops 2877292544 | bytes 16859136 | tf_op jit(solution)/shard_map/mrk,mrc->kc/dot_general | solution.py:82
  299.5 122.0 %reduce-scatter.3.cloned.1.call-done = f32[896,896]{1,0:T(8,128)} async-done(((f32[3584,896]{1,0:T(8,128)}), f32[896,896]{1,0:T(8,128)}) %reduce-scatter.3.cloned.1.call-update) | async-done | bytes 3211280 | tf_op jit(solution)/shard_map/reduce_scatter | solution.py:14
  421.5 3.8 constant_dynamic-slice_fusion.1
  425.3 2.8 gather_fusion
  428.8 41.6 %reduce-scatter.5.cloned.1.call-done = f32[112,896]{1,0:T(8,128)} async-done(((f32[896,896]{1,0:T(8,128)}), f32[112,896]{1,0:T(8,128)}) %reduce-scatter.5.cloned.1.call-update) | async-done | bytes 401424 | tf_op jit(solution)/shard_map/reduce_scatter | solution.py:14
  472.4 33.7 %convert_reduce_fusion = f32[112,3584]{1,0:T(8,128)S(1)} fusion(bf16[4,112,3584]{0,2,1:T(8,128)(2,1)} %constant_dynamic-update-slice_fusion), kind=kLoop, calls=%fused_computation.2 | loop fusion | flops 2809856 | bytes 4816896 | tf_op jit(solution)/shard_map/reduce_sum | solution.py:74
  507.9 54.5 %all-gather.3.cloned.1.call-done = bf16[3584,896]{1,0:T(8,128)(2,1)} async-done(((bf16[112,896]{1,0:T(8,128)(2,1)}), bf16[3584,896]{1,0:T(8,128)(2,1)}) %all-gather.3.cloned.1.call-update) | async-done | bytes 6422544 | tf_op jit(solution)/shard_map/all_gather | solution.py:91
  562.4 6.6 multiply_reduce_fusion.6
  569.2 21.5 %all_to_all.12 = f32[32,1,3584]{2,1,0:T(1,128)S(1)} all-to-all(f32[32,1,3584]{2,1,0:T(1,128)S(1)} %broadcast_in_dim.15), channel_id=1, replica_groups=mesh['row_0'=4,'row_1'=8,'col'=8] {'row_0','row_1'}, dimensions={0} | all-to-all | bytes 917504 | tf_op jit(solution)/shard_map/all_to_all | solution.py:20
  592.8 84.9 %all-gather.5.cloned.1.call-done = bf16[3584,896]{1,0:T(8,128)(2,1)} async-done(((bf16[112,896]{1,0:T(8,128)(2,1)}), bf16[3584,896]{1,0:T(8,128)(2,1)}) %all-gather.5.cloned.1.call-update) | async-done | bytes 6422544 | tf_op jit(solution)/shard_map/all_gather | solution.py:91
  677.7 6.7 multiply_reduce_fusion.3
  684.7 21.5 %all_to_all.13 = f32[32,1,3584]{2,1,0:T(1,128)S(1)} all-to-all(f32[32,1,3584]{2,1,0:T(1,128)S(1)} %broadcast_in_dim.16), channel_id=1, replica_groups=mesh['row_0'=4,'row_1'=8,'col'=8] {'row_0','row_1'}, dimensions={0} | all-to-all | bytes 917504 | tf_op jit(solution)/shard_map/all_to_all | solution.py:20
  (42 shorter events, 12.2 us)
Async XLA Ops:
  7.2 283.5 %copy-start = (bf16[4,112,896]{2,1,0:T(8,128)(2,1)S(1)}, bf16[4,112,896]{2,1,0:T(8,128)(2,1)}, u32[]{:S(2)}) copy-start(bf16[4,112,896]{2,1,0:T(8,128)(2,1)} %param.3) | copy-start | bytes 2408452
  7.2 414.2 %reduce-scatter.3.cloned.1.call-start = ((), (), s32[]{:S(2)}) async-start(), calls=%async_computation.4 | async-start | bytes 16056320 | tf_op jit(solution)/shard_map/reduce_scatter | solution.py:14
  7.2 54.6 %collective-permute-start = (bf16[4,112,448]{2,1,0:T(8,128)(2,1)}, bf16[4,112,448]{2,1,0:T(8,128)(2,1)S(1)}, u32[]{:S(2)}, u32[]{:S(2)}) collective-permute-start(bf16[4,112,448]{2,1,0:T(8,128)(2,1)} %param.2), channel_id=1, source_target_pairs={{0,1},{1,2},{2,3},{3,4},{4,5},{5,6},{6,7},{7,0},{8,9},{9,10},{10,1... | collective-permute-start | bytes 1204232 | tf_op jit(solution)/shard_map/ppermute | solution.py:54
  7.2 75.2 %collective-permute-start.1 = (bf16[4,112,448]{2,1,0:T(8,128)(2,1)}, bf16[4,112,448]{2,1,0:T(8,128)(2,1)S(1)}, u32[]{:S(2)}, u32[]{:S(2)}) collective-permute-start(bf16[4,112,448]{2,1,0:T(8,128)(2,1)} %param.2), channel_id=1, source_target_pairs={{0,7},{1,0},{2,1},{3,2},{4,3},{5,4},{6,5},{7,6},{8,15},{9,8},{10,9... | collective-permute-start | bytes 1204232 | tf_op jit(solution)/shard_map/ppermute | solution.py:62
  21.0 35.4 %copy-start.1 = (bf16[4,112,448]{0,2,1:T(8,128)(2,1)S(1)}, bf16[4,112,448]{0,2,1:T(8,128)(2,1)}, u32[]{:S(2)}) copy-start(bf16[4,112,448]{0,2,1:T(8,128)(2,1)} %copy.30) | copy-start | bytes 1204228
  82.4 23.6 %collective-permute-start.2 = (bf16[4,112,448]{2,1,0:T(8,128)(2,1)S(1)}, bf16[4,112,448]{2,1,0:T(8,128)(2,1)S(1)}, u32[]{:S(2)}, u32[]{:S(2)}) collective-permute-start(bf16[4,112,448]{2,1,0:T(8,128)(2,1)S(1)} %collective-permute-done), channel_id=1, source_target_pairs={{0,1},{1,2},{2,3},{3,4},{4,5},{5,6},{6,7},{7,0},{8,9},{9,10},{10,1... | collective-permute-start | bytes 1204232 | tf_op jit(solution)/shard_map/ppermute | solution.py:54
  103.0 23.6 %collective-permute-start.3 = (bf16[4,112,448]{2,1,0:T(8,128)(2,1)S(1)}, bf16[4,112,448]{2,1,0:T(8,128)(2,1)S(1)}, u32[]{:S(2)}, u32[]{:S(2)}) collective-permute-start(bf16[4,112,448]{2,1,0:T(8,128)(2,1)S(1)} %collective-permute-done.1), channel_id=1, source_target_pairs={{0,7},{1,0},{2,1},{3,2},{4,3},{5,4},{6,5},{7,6},{8,15},{9,8},{10,9... | collective-permute-start | bytes 1204232 | tf_op jit(solution)/shard_map/ppermute | solution.py:62
  126.6 23.5 %collective-permute-start.4 = (bf16[4,112,448]{2,1,0:T(8,128)(2,1)S(1)}, bf16[4,112,448]{2,1,0:T(8,128)(2,1)S(1)}, u32[]{:S(2)}, u32[]{:S(2)}) collective-permute-start(bf16[4,112,448]{2,1,0:T(8,128)(2,1)S(1)} %collective-permute-done.2), channel_id=1, source_target_pairs={{0,1},{1,2},{2,3},{3,4},{4,5},{5,6},{6,7},{7,0},{8,9},{9,10},{10,1... | collective-permute-start | bytes 1204232 | tf_op jit(solution)/shard_map/ppermute | solution.py:54
  147.3 23.4 %collective-permute-start.5 = (bf16[4,112,448]{2,1,0:T(8,128)(2,1)S(1)}, bf16[4,112,448]{2,1,0:T(8,128)(2,1)S(1)}, u32[]{:S(2)}, u32[]{:S(2)}) collective-permute-start(bf16[4,112,448]{2,1,0:T(8,128)(2,1)S(1)} %collective-permute-done.3), channel_id=1, source_target_pairs={{0,7},{1,0},{2,1},{3,2},{4,3},{5,4},{6,5},{7,6},{8,15},{9,8},{10,9... | collective-permute-start | bytes 1204232 | tf_op jit(solution)/shard_map/ppermute | solution.py:62
  170.8 20.7 %collective-permute-start.6 = (bf16[4,112,448]{2,1,0:T(8,128)(2,1)S(1)}, bf16[4,112,448]{2,1,0:T(8,128)(2,1)S(1)}, u32[]{:S(2)}, u32[]{:S(2)}) collective-permute-start(bf16[4,112,448]{2,1,0:T(8,128)(2,1)S(1)} %collective-permute-done.4), channel_id=1, source_target_pairs={{0,1},{1,2},{2,3},{3,4},{4,5},{5,6},{6,7},{7,0},{8,9},{9,10},{10,1... | collective-permute-start | bytes 1204232 | tf_op jit(solution)/shard_map/ppermute | solution.py:54
  299.4 171.0 %reduce-scatter.5.cloned.1.call-start = ((), (), s32[]{:S(2)}) async-start(), calls=%async_computation.5 | async-start | bytes 3612672 | tf_op jit(solution)/shard_map/reduce_scatter | solution.py:14
  421.4 140.9 %all-gather.3.cloned.1.call-start = ((), (), s32[]{:S(2)}) async-start(), calls=%async_computation.6 | async-start | bytes 6623232 | tf_op jit(solution)/shard_map/all_gather | solution.py:91
  472.2 90.2 %copy-start.2 = (bf16[112,896]{1,0:T(8,128)(2,1)S(1)}, bf16[112,896]{1,0:T(8,128)(2,1)}, u32[]{:S(2)}) copy-start(bf16[112,896]{1,0:T(8,128)(2,1)} %get-tuple-element.13) | copy-start | bytes 602116
  472.2 205.6 %all-gather.5.cloned.1.call-start = ((), (), s32[]{:S(2)}) async-start(), calls=%async_computation.7 | async-start | bytes 6623232 | tf_op jit(solution)/shard_map/all_gather | solution.py:91
Sparse Core Ops, SparseCore 0:
  299.5 121.8 reduce-scatter.2
  424.0 46.3 reduce-scatter.4
  473.6 88.7 all-gather.2
  593.0 84.7 all-gather.4
